TPU v7x, 32 devices: a whole 2x2x4 slice. The times are simulated.
32 devices in a mesh: px: 4 (over z), py: 4 (over y, x), pz: 2 (over core).
Axes of the slice: x: 2, y: 2, z: 4, core: 2. Of those that a mesh axis runs over, the one named last changes fastest.
Arguments:
- right_side: float32 [16, 64, 256], P('px', 'py', 'pz'), may hold values from -160 to 160
- start_guess: float32 [16, 64, 256], P('px', 'py', 'pz'), may hold values from -4 to 4
- conductivity: float32 [16, 64, 256], P('px', 'py', 'pz'), may hold values from 0.05 to 0.4
- recycled: float32 [16, 16, 64, 256], P(None, 'px', 'py', 'pz'), may hold values from -6 to 6
Outputs:
- solution: float32 [16, 64, 256], P('px', 'py', 'pz')
- residual: float32 [16, 64, 256], P('px', 'py', 'pz')
- hessenberg: float32 [9, 8], replicated
All inputs are finite; a program needn't handle non-finite values.
Results may differ from a plain program's by a relative error of at most 0.03.
Values sent between devices are 32-bit elements; how exact they have to be, the bound alone decides.
A program may use at most 128 MiB of HBM per device.

v0:
```python
import jax
import jax.numpy as jnp
from jax import lax
from jax.sharding import PartitionSpec as P

STEPS = 8
highest = lax.Precision.HIGHEST
edge_weight = 0.25 ** (1.0 / 3.0)
middle_weight = 2.0 * edge_weight
shift_value = 0.4


def padded_2(array, sides, width):
    for axis, dim in sides:
        peers, length = (lax.axis_size(axis), array.shape[dim])
        up = [(i, (i + 1) % peers) for i in range(peers - 1)]
        down = [(j, i) for i, j in up]
        last = lax.slice_in_dim(array, length - width, length, axis=dim)
        leading = lax.slice_in_dim(array, 0, width, axis=dim)
        before = lax.ppermute(last, axis, up)
        after = lax.ppermute(leading, axis, down)
        array = jnp.concatenate([before, array, after], axis=dim)
    return array


def stencil_sum(padded):
    along_z = edge_weight * (padded[..., :-2] + padded[..., 2:]) + middle_weight * padded[..., 1:-1]
    along_y = (
        edge_weight * (along_z[..., :-2, :] + along_z[..., 2:, :])
        + middle_weight * along_z[..., 1:-1, :]
    )
    along_x = (
        edge_weight * (along_y[..., :-2, :, :] + along_y[..., 2:, :, :])
        + middle_weight * along_y[..., 1:-1, :, :]
    )
    return along_x - 2.0 * padded[..., 1:-1, 1:-1, 1:-1]


def apply_batch(fields, conductivity, diagonal):
    stacked = jnp.concatenate((fields, conductivity[None] * fields), axis=0)
    padded = padded_2(stacked, (("px", 1), ("py", 2), ("pz", 3)), 1)
    half_count = fields.shape[0]
    near_sum = stencil_sum(padded[:half_count])
    far_sum = stencil_sum(padded[half_count:])
    return diagonal * fields - 0.5 * conductivity * near_sum - 0.5 * far_sum


def apply_vector(fields, conductivity, diagonal):
    stacked = jnp.concatenate((fields, conductivity[None] * fields), axis=0)
    padded = padded_2(stacked, (("px", 1), ("py", 2), ("pz", 3)), 1)
    near_sum = stencil_sum(padded[:1])
    far_sum = stencil_sum(padded[1:])
    return diagonal * fields - 0.5 * conductivity * near_sum - 0.5 * far_sum


def cholesky_low(gram):
    order = gram.shape[0]
    rows_idx = jnp.arange(order)
    factor = jnp.zeros((order, order), jnp.float32)
    for column in range(order):
        known = factor[:, :column]
        partial_sum = jnp.sum(known * known[column][None, :], axis=1)
        pivot = jnp.sqrt(gram[column, column] - partial_sum[column])
        values = (gram[:, column] - partial_sum) / pivot
        values = jnp.where(rows_idx > column, values, 0.0)
        factor = factor.at[:, column].set(values).at[column, column].set(pivot)
    return factor


def lower_inverse(factor):
    order = factor.shape[0]
    inverse = jnp.zeros((order, order), jnp.float32)
    for row in range(order):
        unit_row = jnp.zeros((order,), jnp.float32).at[row].set(1.0)
        partial_value = jnp.sum(factor[row, :row][:, None] * inverse[:row], axis=0)
        inverse = inverse.at[row].set((unit_row - partial_value) / factor[row, row])
    return inverse


def back_solve(upper_tri, target):
    order = upper_tri.shape[0]
    result = jnp.zeros((order,), jnp.float32)
    for row in range(order - 1, -1, -1):
        partial_value = jnp.sum(upper_tri[row, row + 1 :] * result[row + 1 :])
        result = result.at[row].set((target[row] - partial_value) / upper_tri[row, row])
    return result


def least_squares(hessenberg, beta_norm):
    upper_tri = hessenberg
    target = jnp.zeros((STEPS + 1,), jnp.float32).at[0].set(beta_norm)
    for column in range(STEPS):
        top_entry = upper_tri[column, column]
        low_entry = upper_tri[column + 1, column]
        radius = jnp.sqrt(top_entry * top_entry + low_entry * low_entry)
        cosine = top_entry / radius
        sine_val = low_entry / radius
        row_top = cosine * upper_tri[column] + sine_val * upper_tri[column + 1]
        row_low = cosine * upper_tri[column + 1] - sine_val * upper_tri[column]
        upper_tri = upper_tri.at[column].set(row_top).at[column + 1].set(row_low)
        goal_top = cosine * target[column] + sine_val * target[column + 1]
        goal_low = cosine * target[column + 1] - sine_val * target[column]
        target = target.at[column].set(goal_top).at[column + 1].set(goal_low)
    return back_solve(upper_tri[:STEPS], target[:STEPS])


def body(right_side, start_guess, conductivity, recycled):
    count_k = recycled.shape[0]
    block_shape = right_side.shape
    cell_count = right_side.size
    padded_cond = padded_2(conductivity, (("px", 0), ("py", 1), ("pz", 2)), 1)
    diagonal = shift_value + 7.0 * conductivity + 0.5 * stencil_sum(padded_cond)
    batch_in = jnp.concatenate((recycled, start_guess[None]), axis=0)
    images_all = apply_batch(batch_in, conductivity, diagonal)
    flat_images = images_all[:count_k].reshape(count_k, cell_count)
    first_residual = right_side.reshape(cell_count) - images_all[count_k].reshape(cell_count)
    gram = lax.psum(jnp.dot(flat_images, flat_images.T, precision=highest), ("px", "py", "pz"))
    factor_low = cholesky_low(gram)
    inverse = lower_inverse(factor_low)
    basis_c = jnp.dot(inverse, flat_images, precision=highest)
    projected = lax.psum(jnp.dot(basis_c, first_residual, precision=highest), ("px", "py", "pz"))
    recycle_flat = recycled.reshape(count_k, cell_count)
    solution = start_guess.reshape(cell_count) + jnp.dot(
        jnp.dot(inverse.T, projected, precision=highest), recycle_flat, precision=highest
    )
    residual = first_residual - jnp.dot(projected, basis_c, precision=highest)
    beta_norm = jnp.sqrt(
        lax.psum(jnp.dot(residual, residual, precision=highest), ("px", "py", "pz"))
    )
    basis_all = jnp.zeros((STEPS + 1, cell_count), jnp.float32).at[0].set(residual / beta_norm)
    coupling = jnp.zeros((count_k, STEPS), jnp.float32)
    hessenberg = jnp.zeros((STEPS + 1, STEPS), jnp.float32)
    for column in range(STEPS):
        current = basis_all[column].reshape((1,) + block_shape)
        vector_new = apply_vector(current, conductivity, diagonal).reshape(cell_count)
        known_basis = basis_all[: column + 1]
        coeff_c, coeff_v, whole_sq = lax.psum(
            (
                jnp.dot(basis_c, vector_new, precision=highest),
                jnp.dot(known_basis, vector_new, precision=highest),
                jnp.dot(vector_new, vector_new, precision=highest),
            ),
            ("px", "py", "pz"),
        )
        vector_new = (
            vector_new
            - jnp.dot(coeff_c, basis_c, precision=highest)
            - jnp.dot(coeff_v, known_basis, precision=highest)
        )
        norm_sq = (
            whole_sq
            - jnp.dot(coeff_c, coeff_c, precision=highest)
            - jnp.dot(coeff_v, coeff_v, precision=highest)
        )
        norm_new = jnp.sqrt(norm_sq)
        coupling = coupling.at[:, column].set(coeff_c)
        hessenberg = hessenberg.at[: column + 1, column].set(coeff_v)
        hessenberg = hessenberg.at[column + 1, column].set(norm_new)
        basis_all = basis_all.at[column + 1].set(vector_new / norm_new)
    coeffs = least_squares(hessenberg, beta_norm)
    recycle_coeffs = jnp.dot(
        inverse.T, jnp.dot(coupling, coeffs, precision=highest), precision=highest
    )
    solution = (
        solution
        + jnp.dot(coeffs, basis_all[:STEPS], precision=highest)
        - jnp.dot(recycle_coeffs, recycle_flat, precision=highest)
    )
    residual = residual - jnp.dot(
        jnp.dot(hessenberg, coeffs, precision=highest), basis_all, precision=highest
    )
    return (solution.reshape(block_shape), residual.reshape(block_shape), hessenberg)


def solution(mesh):
    return jax.shard_map(
        body,
        mesh=mesh,
        in_specs=(
            P("px", "py", "pz"),
            P("px", "py", "pz"),
            P("px", "py", "pz"),
            P(None, "px", "py", "pz"),
        ),
        out_specs=(P("px", "py", "pz"), P("px", "py", "pz"), P()),
        check_vma=False,
    )
```

profile of v0, /device:TPU:0, one launch (start us, length us, event | category | flops | bytes accessed | tf_op | source)
XLA Modules:
  0.0 911.4 jit_solution(14122070898462380592)
XLA Ops:
  3.0 5.0 collective-permute-start.6
  9.3 4.5 collective-permute-start
  19.5 3.4 collective-permute-start.2
  37.9 4.6 collective-permute-start.8
  46.0 5.5 collective-permute-done.9
  52.4 2.7 fusion.321
  55.1 3.1 copy.40
  58.2 2.6 collective-permute-start.10
  60.8 3.1 copy.42
  66.7 3.1 copy.41
  69.8 3.0 copy.43
  72.8 6.4 maximum_maximum_fusion
  82.7 42.2 %psum.189 = f32[16,16]{1,0:T(8,128)S(1)} all-reduce(f32[16,16]{1,0:T(8,128)S(1)} %convolution_bitcast_fusion), channel_id=1, replica_groups=mesh['px'=4,'py'=4,'pz'=2] {'px','py','pz'}, use_global_device_ids=true, to_apply=%region_1.2 | all-reduce | flops 256 | bytes 2048 | tf_op jit(solution)/shard_map/psum | solution.py:117
  187.5 39.8 %psum.190 = f32[16]{0:T(128)S(1)} all-reduce(f32[16]{0:T(128)S(1)} %convolution_bitcast_fusion.20), channel_id=1, replica_groups=mesh['px'=4,'py'=4,'pz'=2] {'px','py','pz'}, use_global_device_ids=true, to_apply=%region_44.45 | all-reduce | flops 16 | bytes 128 | tf_op jit(solution)/shard_map/psum | solution.py:121
  228.2 40.2 %psum.191 = f32[]{:T(128)} all-reduce(f32[]{:T(128)} %get-tuple-element.1699), channel_id=1, replica_groups=mesh['px'=4,'py'=4,'pz'=2] {'px','py','pz'}, use_global_device_ids=true, to_apply=%region_45.46 | all-reduce | flops 1 | bytes 8 | tf_op jit(solution)/shard_map/psum | solution.py:128
  269.2 3.6 collective-permute-start.12
  274.7 3.7 collective-permute-done.13
  278.5 4.2 collective-permute-start.14
  284.0 4.2 collective-permute-done.15
  295.2 40.4 %all-reduce.14 = (f32[16]{0:T(128)S(1)}, f32[]{:T(128)}, f32[1]{0:T(128)}) all-reduce(f32[16]{0:T(128)S(1)} %convolution_bitcast_fusion.19, f32[]{:T(128)} %get-tuple-element.1697, f32[1]{0:T(128)} %bitcast.135), channel_id=1, replica_groups=mesh['px'=4,'py'=4,'pz'=2] {'px','py','pz'}, use_global_device_ids=true, to_apply=%region_48.49 | all-reduce | flops 18 | bytes 144 | tf_op jit(solution)/shard_map/psum | solution.py:137
  344.4 4.2 collective-permute-done.19
  348.7 4.2 collective-permute-start.20
  354.8 3.6 collective-permute-done.21
  365.5 39.3 %all-reduce.13 = (f32[16]{0:T(128)S(1)}, f32[2]{0:T(128)S(1)}, f32[]{:T(128)}) all-reduce(f32[16]{0:T(128)S(1)} %convolution_bitcast_fusion.17, f32[2]{0:T(128)S(1)} %convolution_bitcast_fusion.18, f32[]{:T(128)} %get-tuple-element.1695), channel_id=1, replica_groups=mesh['px'=4,'py'=4,'pz'=2] {'px','py','pz'}, use_global_device_ids=true, to_apply=%region_52.53 | all-reduce | flops 19 | bytes 152 | tf_op jit(solution)/shard_map/psum | solution.py:137
  409.4 3.2 collective-permute-start.24
  414.5 3.7 collective-permute-done.25
  418.3 4.2 collective-permute-start.26
  423.8 4.2 collective-permute-done.27
  435.1 39.3 %all-reduce.12 = (f32[16]{0:T(128)S(1)}, f32[3]{0:T(128)S(1)}, f32[]{:T(128)}) all-reduce(f32[16]{0:T(128)S(1)} %convolution_bitcast_fusion.15, f32[3]{0:T(128)S(1)} %convolution_bitcast_fusion.16, f32[]{:T(128)} %get-tuple-element.1693), channel_id=1, replica_groups=mesh['px'=4,'py'=4,'pz'=2] {'px','py','pz'}, use_global_device_ids=true, to_apply=%region_56.57 | all-reduce | flops 20 | bytes 160 | tf_op jit(solution)/shard_map/psum | solution.py:137
  478.4 3.2 collective-permute-start.30
  483.0 4.2 collective-permute-done.31
  487.3 4.2 collective-permute-start.32
  504.3 41.2 %all-reduce.11 = (f32[16]{0:T(128)S(1)}, f32[4]{0:T(128)S(1)}, f32[]{:T(128)}) all-reduce(f32[16]{0:T(128)S(1)} %convolution_bitcast_fusion.13, f32[4]{0:T(128)S(1)} %convolution_bitcast_fusion.14, f32[]{:T(128)} %get-tuple-element.1691), channel_id=1, replica_groups=mesh['px'=4,'py'=4,'pz'=2] {'px','py','pz'}, use_global_device_ids=true, to_apply=%region_60.61 | all-reduce | flops 21 | bytes 168 | tf_op jit(solution)/shard_map/psum | solution.py:137
  549.4 3.2 collective-permute-start.36
  555.4 2.8 collective-permute-done.37
  558.3 4.2 collective-permute-start.38
  575.1 40.1 %all-reduce.10 = (f32[16]{0:T(128)S(1)}, f32[5]{0:T(128)S(1)}, f32[]{:T(128)}) all-reduce(f32[16]{0:T(128)S(1)} %convolution_bitcast_fusion.11, f32[5]{0:T(128)S(1)} %convolution_bitcast_fusion.12, f32[]{:T(128)} %get-tuple-element.1689), channel_id=1, replica_groups=mesh['px'=4,'py'=4,'pz'=2] {'px','py','pz'}, use_global_device_ids=true, to_apply=%region_64.65 | all-reduce | flops 22 | bytes 176 | tf_op jit(solution)/shard_map/psum | solution.py:137
  619.1 3.2 collective-permute-start.42
  627.9 4.2 collective-permute-start.44
  634.1 3.6 collective-permute-done.45
  646.5 41.4 %all-reduce.9 = (f32[16]{0:T(128)S(1)}, f32[6]{0:T(128)S(1)}, f32[]{:T(128)}) all-reduce(f32[16]{0:T(128)S(1)} %convolution_bitcast_fusion.9, f32[6]{0:T(128)S(1)} %convolution_bitcast_fusion.10, f32[]{:T(128)} %get-tuple-element.1687), channel_id=1, replica_groups=mesh['px'=4,'py'=4,'pz'=2] {'px','py','pz'}, use_global_device_ids=true, to_apply=%region_68.69 | all-reduce | flops 23 | bytes 184 | tf_op jit(solution)/shard_map/psum | solution.py:137
  691.8 2.6 collective-permute-start.48
  696.4 3.7 collective-permute-done.49
  700.1 4.2 collective-permute-start.50
  717.0 40.6 %all-reduce.8 = (f32[16]{0:T(128)S(1)}, f32[7]{0:T(128)S(1)}, f32[]{:T(128)}) all-reduce(f32[16]{0:T(128)S(1)} %convolution_bitcast_fusion.7, f32[7]{0:T(128)S(1)} %convolution_bitcast_fusion.8, f32[]{:T(128)} %get-tuple-element.1685), channel_id=1, replica_groups=mesh['px'=4,'py'=4,'pz'=2] {'px','py','pz'}, use_global_device_ids=true, to_apply=%region_72.73 | all-reduce | flops 24 | bytes 192 | tf_op jit(solution)/shard_map/psum | solution.py:137
  769.7 4.2 collective-permute-start.56
  775.8 3.6 collective-permute-done.57
  788.4 41.4 %all-reduce.7 = (f32[16]{0:T(128)S(1)}, f32[8]{0:T(128)S(1)}, f32[]{:T(128)}) all-reduce(f32[16]{0:T(128)S(1)} %convolution_bitcast_fusion.5, f32[8]{0:T(128)S(1)} %convolution_bitcast_fusion.6, f32[]{:T(128)} %get-tuple-element.1683), channel_id=1, replica_groups=mesh['px'=4,'py'=4,'pz'=2] {'px','py','pz'}, use_global_device_ids=true, to_apply=%region_76.77 | all-reduce | flops 25 | bytes 200 | tf_op jit(solution)/shard_map/psum | solution.py:137
  (649 shorter events, 233.4 us)
Async XLA Ops:
  3.0 34.8 %collective-permute-start.6 = (f32[34,1,16,128]{3,0,2,1:T(8,128)S(1)}, f32[34,1,16,128]{3,0,2,1:T(8,128)S(1)}, u32[]{:S(2)}, u32[]{:S(2)}) collective-permute-start(f32[34,1,16,128]{3,0,2,1:T(8,128)S(1)} %get-tuple-element.1711), channel_id=1, source_target_pairs={{0,8},{8,16},{16,24},{1,9},{9,17},{17,25},{2,10},{10,18},{18,26},{... | collective-permute-start | bytes 835592 | tf_op jit(solution)/shard_map/ppermute | solution.py:20
  8.0 29.9 %collective-permute-start.7 = (f32[34,1,16,128]{3,0,2,1:T(8,128)S(1)}, f32[34,1,16,128]{3,0,2,1:T(8,128)S(1)}, u32[]{:S(2)}, u32[]{:S(2)}) collective-permute-start(f32[34,1,16,128]{3,0,2,1:T(8,128)S(1)} %get-tuple-element.1712), channel_id=1, source_target_pairs={{8,0},{16,8},{24,16},{9,1},{17,9},{25,17},{10,2},{18,10},{26,18},{... | collective-permute-start | bytes 835592 | tf_op jit(solution)/shard_map/ppermute | solution.py:21
  9.3 10.0 %collective-permute-start = (f32[1,16,128]{2,1,0:T(8,128)S(1)}, f32[1,16,128]{2,1,0:T(8,128)S(1)}, u32[]{:S(2)}, u32[]{:S(2)}) collective-permute-start(f32[1,16,128]{2,1,0:T(8,128)S(1)} %get-tuple-element.1768), channel_id=1, source_target_pairs={{0,8},{8,16},{16,24},{1,9},{9,17},{17,25},{2,10},{10,18},{18,26},{... | collective-permute-start | bytes 24584 | tf_op jit(solution)/shard_map/ppermute | solution.py:20
  13.9 5.5 collective-permute-start.1
  19.5 12.8 %collective-permute-start.2 = (f32[6,1,128]{2,1,0:T(1,128)S(1)}, f32[6,1,128]{2,1,0:T(1,128)S(1)}, u32[]{:S(2)}, u32[]{:S(2)}) collective-permute-start(f32[6,1,128]{2,1,0:T(1,128)S(1)} %get-tuple-element.1763), channel_id=1, source_target_pairs={{0,2},{2,4},{4,6},{1,3},{3,5},{5,7},{8,10},{10,12},{12,14},{9,11},... | collective-permute-start | bytes 9224 | tf_op jit(solution)/shard_map/ppermute | solution.py:20
  22.9 9.4 %collective-permute-start.3 = (f32[6,1,128]{2,1,0:T(1,128)S(1)}, f32[6,1,128]{2,1,0:T(1,128)S(1)}, u32[]{:S(2)}, u32[]{:S(2)}) collective-permute-start(f32[6,1,128]{2,1,0:T(1,128)S(1)} %get-tuple-element.1764), channel_id=1, source_target_pairs={{2,0},{4,2},{6,4},{3,1},{5,3},{7,5},{10,8},{12,10},{14,12},{11,9},... | collective-permute-start | bytes 9224 | tf_op jit(solution)/shard_map/ppermute | solution.py:21
  32.4 5.3 collective-permute-start.4
  33.7 4.0 collective-permute-start.5
  37.9 8.1 collective-permute-start.8
  42.5 9.0 collective-permute-start.9
  58.2 8.5 collective-permute-start.10
  63.9 5.9 collective-permute-start.11
  269.2 5.5 collective-permute-start.12
  272.8 5.6 collective-permute-start.13
  278.5 5.5 collective-permute-start.14
  282.6 5.5 collective-permute-start.15
  288.3 3.9 collective-permute-start.16
  343.0 5.6 collective-permute-start.19
  348.7 6.2 collective-permute-start.20
  352.9 5.5 collective-permute-start.21
  409.4 5.1 collective-permute-start.24
  412.6 5.6 collective-permute-start.25
  418.3 5.5 collective-permute-start.26
  422.5 5.5 collective-permute-start.27
  478.4 4.6 collective-permute-start.30
  481.6 5.6 collective-permute-start.31
  487.3 9.5 %collective-permute-start.32 = (f32[2,6,1,128]{3,2,1,0:T(1,128)S(1)}, f32[2,6,1,128]{3,2,1,0:T(1,128)S(1)}, u32[]{:S(2)}, u32[]{:S(2)}) collective-permute-start(f32[2,6,1,128]{3,2,1,0:T(1,128)S(1)} %get-tuple-element.1737), channel_id=1, source_target_pairs={{0,2},{2,4},{4,6},{1,3},{3,5},{5,7},{8,10},{10,12},{12,14},{9,11},... | collective-permute-start | bytes 18440 | tf_op jit(solution)/shard_map/ppermute | solution.py:20
  491.4 5.5 collective-permute-start.33
  549.4 6.0 collective-permute-start.36
  552.6 5.6 collective-permute-start.37
  558.3 9.1 %collective-permute-start.38 = (f32[2,6,1,128]{3,2,1,0:T(1,128)S(1)}, f32[2,6,1,128]{3,2,1,0:T(1,128)S(1)}, u32[]{:S(2)}, u32[]{:S(2)}) collective-permute-start(f32[2,6,1,128]{3,2,1,0:T(1,128)S(1)} %get-tuple-element.1735), channel_id=1, source_target_pairs={{0,2},{2,4},{4,6},{1,3},{3,5},{5,7},{8,10},{10,12},{12,14},{9,11},... | collective-permute-start | bytes 18440 | tf_op jit(solution)/shard_map/ppermute | solution.py:20
  562.5 5.5 collective-permute-start.39
  619.1 8.1 collective-permute-start.42
  622.3 5.6 collective-permute-start.43
  627.9 6.1 collective-permute-start.44
  632.1 5.5 collective-permute-start.45
  637.8 6.3 collective-permute-start.46
  639.1 5.0 collective-permute-start.47
  691.8 4.6 collective-permute-start.48
  694.5 5.6 collective-permute-start.49
  700.1 9.1 %collective-permute-start.50 = (f32[2,6,1,128]{3,2,1,0:T(1,128)S(1)}, f32[2,6,1,128]{3,2,1,0:T(1,128)S(1)}, u32[]{:S(2)}, u32[]{:S(2)}) collective-permute-start(f32[2,6,1,128]{3,2,1,0:T(1,128)S(1)} %get-tuple-element.1731), channel_id=1, source_target_pairs={{0,2},{2,4},{4,6},{1,3},{3,5},{5,7},{8,10},{10,12},{12,14},{9,11},... | collective-permute-start | bytes 18440 | tf_op jit(solution)/shard_map/ppermute | solution.py:20
  704.3 5.5 collective-permute-start.51
  761.5 7.4 collective-permute-start.54
  764.0 5.6 collective-permute-start.55
  769.7 6.1 collective-permute-start.56
  773.9 5.5 collective-permute-start.57
  779.5 6.4 collective-permute-start.58
  780.8 5.1 collective-permute-start.59
  (46 other events, 2003.3 us)
where the time goes:
time: 925 us; the launch traced here: 911 us
  blocking collectives  446 us (48%)
  starting transfers between devices  128 us (14%)
  other arithmetic  98.5 us (11%)
  between operations  91.1 us (10%)
  local copies, waits for them, and re-layouts  68.2 us (7%)
  waiting for transfers between devices  58.2 us (6%)
  matrix products  21.4 us (2%)
    psum x8, blocking collectives, body(): lax.psum((jnp.dot(basis_c, vector_new, precision=highest), jnp.dot(known_...  324 us
    ppermute x30, starting transfers between devices, padded_2(): before = lax.ppermute(last, axis, up)  89.3 us
    ppermute x30, waiting for transfers between devices, padded_2(): after = lax.ppermute(leading, axis, down)  56.3 us
    another operation x61, other arithmetic  46.9 us
    psum x1, blocking collectives, body(): lax.psum(jnp.dot(flat_images, flat_images.T, precision=highest), ('px', '...  42.2 us
    psum x1, blocking collectives, body(): lax.psum(jnp.dot(residual, residual, precision=highest), ('px', 'py', 'pz'))  40.2 us
    psum x1, blocking collectives, body(): lax.psum(jnp.dot(basis_c, first_residual, precision=highest), ('px', 'py'...  39.8 us
    ppermute x30, starting transfers between devices, padded_2(): after = lax.ppermute(leading, axis, down)  38.8 us
  transfers between devices with their start and end apart: 60, of which 27 were waited for; matrix products, arithmetic and copies ran while one was open for 7% of the time, Pallas kernels for 0%

commit v1 on v0

--- a/solution.py
+++ b/solution.py
@@ -135,12 +135,15 @@
         vector_new = apply_vector(current, conductivity, diagonal).reshape(cell_count)
         known_basis = basis_all[: column + 1]
         coeff_c, coeff_v, whole_sq = lax.psum(
-            (
-                jnp.dot(basis_c, vector_new, precision=highest),
-                jnp.dot(known_basis, vector_new, precision=highest),
-                jnp.dot(vector_new, vector_new, precision=highest),
+            lax.psum(
+                (
+                    jnp.dot(basis_c, vector_new, precision=highest),
+                    jnp.dot(known_basis, vector_new, precision=highest),
+                    jnp.dot(vector_new, vector_new, precision=highest),
+                ),
+                ("py", "pz"),
             ),
-            ("px", "py", "pz"),
+            "px",
         )
         vector_new = (
             vector_new

time: 925 us -> 793 us (0.86)
  blocking collectives: 446 us -> 309 us
  waiting for transfers between devices: 58.2 us -> 71.4 us
    psum x8, blocking collectives: 324 us -> 108 us  [body(): lax.psum((jnp.dot(basis_c, vector_new, precision=highest), jnp.dot(known_...]
    psum x0 -> x8, blocking collectives: none -> 78.1 us  [body(): lax.psum(lax.psum((jnp.dot(basis_c, vector_new, precision=highest), jnp.d...]
    ppermute x30, waiting for transfers between devices: 56.3 us -> 69.5 us  [padded_2(): after = lax.ppermute(leading, axis, down)]
  transfers between devices with their start and end apart: 60 -> 60, of which waited for: 27 -> 27; matrix products, arithmetic and copies ran while one was open for 7% -> 8% of each run, Pallas kernels for 0% -> 0%
where the time goes in v1:
time: 793 us; the launch traced here: 779 us
  blocking collectives  309 us (39%)
  starting transfers between devices  120 us (15%)
  other arithmetic  98.3 us (12%)
  between operations  91.2 us (12%)
  waiting for transfers between devices  71.4 us (9%)
  local copies, waits for them, and re-layouts  67.8 us (9%)
  matrix products  21.4 us (3%)
    psum x8, blocking collectives, body(): lax.psum((jnp.dot(basis_c, vector_new, precision=highest), jnp.dot(known_...  108 us
    ppermute x30, starting transfers between devices, padded_2(): before = lax.ppermute(last, axis, up)  80.9 us
    psum x8, blocking collectives, body(): lax.psum(lax.psum((jnp.dot(basis_c, vector_new, precision=highest), jnp.d...  78.1 us
    ppermute x30, waiting for transfers between devices, padded_2(): after = lax.ppermute(leading, axis, down)  69.5 us
    another operation x61, other arithmetic  46.8 us
    psum x1, blocking collectives, body(): lax.psum(jnp.dot(flat_images, flat_images.T, precision=highest), ('px', '...  42.2 us
    psum x1, blocking collectives, body(): lax.psum(jnp.dot(residual, residual, precision=highest), ('px', 'py', 'pz'))  40.3 us
    psum x1, blocking collectives, body(): lax.psum(jnp.dot(basis_c, first_residual, precision=highest), ('px', 'py'...  39.8 us
  transfers between devices with their start and end apart: 60, of which 27 were waited for; matrix products, arithmetic and copies ran while one was open for 8% of the time, Pallas kernels for 0%

profile of v1, /device:TPU:0, one launch (start us, length us, event | category | flops | bytes accessed | tf_op | source)
XLA Modules:
  0.0 779.1 jit_solution(3895736077826692933)
XLA Ops:
  3.0 5.0 collective-permute-start.6
  9.3 4.5 collective-permute-start
  19.5 3.4 collective-permute-start.2
  37.9 4.6 collective-permute-start.8
  46.0 5.5 collective-permute-done.9
  55.1 3.1 copy.40
  60.8 3.1 copy.42
  72.8 6.4 maximum_maximum_fusion
  82.7 42.2 %psum.357 = f32[16,16]{1,0:T(8,128)S(1)} all-reduce(f32[16,16]{1,0:T(8,128)S(1)} %convolution_bitcast_fusion), channel_id=1, replica_groups=mesh['px'=4,'py'=4,'pz'=2] {'px','py','pz'}, use_global_device_ids=true, to_apply=%region_1.2 | all-reduce | flops 256 | bytes 2048 | tf_op jit(solution)/shard_map/psum | solution.py:117
  187.5 39.8 %psum.358 = f32[16]{0:T(128)S(1)} all-reduce(f32[16]{0:T(128)S(1)} %convolution_bitcast_fusion.20), channel_id=1, replica_groups=mesh['px'=4,'py'=4,'pz'=2] {'px','py','pz'}, use_global_device_ids=true, to_apply=%region_44.45 | all-reduce | flops 16 | bytes 128 | tf_op jit(solution)/shard_map/psum | solution.py:121
  228.3 40.3 %psum.359 = f32[]{:T(128)} all-reduce(f32[]{:T(128)} %get-tuple-element.1723), channel_id=1, replica_groups=mesh['px'=4,'py'=4,'pz'=2] {'px','py','pz'}, use_global_device_ids=true, to_apply=%region_45.46 | all-reduce | flops 1 | bytes 8 | tf_op jit(solution)/shard_map/psum | solution.py:128
  269.2 3.6 collective-permute-start.12
  274.7 3.7 collective-permute-done.13
  278.5 4.2 collective-permute-start.14
  284.0 4.2 collective-permute-done.15
  295.2 12.9 %all-reduce.14 = (f32[16]{0:T(128)S(1)}, f32[]{:T(128)}, f32[1]{0:T(128)}) all-reduce(f32[16]{0:T(128)S(1)} %convolution_bitcast_fusion.19, f32[]{:T(128)} %get-tuple-element.1721, f32[1]{0:T(128)} %bitcast.135), channel_id=1, replica_groups=mesh['px'=4,'py'=4,'pz'=2] {'py','pz'}, use_global_device_ids=true, to_apply=%region_50.51 | all-reduce | flops 18 | bytes 144 | tf_op jit(solution)/shard_map/psum | solution.py:138
  308.2 10.4 %all-reduce.22 = (f32[16]{0:T(128)S(1)}, f32[]{:T(128)}, f32[1]{0:T(128)}) all-reduce(f32[16]{0:T(128)S(1)} %get-tuple-element.1680, f32[]{:T(128)} %get-tuple-element.1681, f32[1]{0:T(128)} %get-tuple-element.1682), channel_id=1, replica_groups=mesh['px'=4,'py'=4,'pz'=2] {'px'}, use_global_device_ids=true, to_apply=%region_51.52 | all-reduce | flops 18 | bytes 144 | tf_op jit(solution)/shard_map/psum | solution.py:137
  327.3 4.2 collective-permute-done.19
  331.6 3.1 collective-permute-start.20
  336.7 5.4 collective-permute-done.21
  349.2 12.7 %all-reduce.13 = (f32[16]{0:T(128)S(1)}, f32[2]{0:T(128)S(1)}, f32[]{:T(128)}) all-reduce(f32[16]{0:T(128)S(1)} %convolution_bitcast_fusion.17, f32[2]{0:T(128)S(1)} %convolution_bitcast_fusion.18, f32[]{:T(128)} %get-tuple-element.1719), channel_id=1, replica_groups=mesh['px'=4,'py'=4,'pz'=2] {'py','pz'}, use_global_device_ids=true, to_apply=%region_57.58 | all-reduce | flops 19 | bytes 152 | tf_op jit(solution)/shard_map/psum | solution.py:138
  361.9 9.0 %all-reduce.21 = (f32[16]{0:T(128)S(1)}, f32[2]{0:T(128)S(1)}, f32[]{:T(128)}) all-reduce(f32[16]{0:T(128)S(1)} %get-tuple-element.1677, f32[2]{0:T(128)S(1)} %get-tuple-element.1678, f32[]{:T(128)} %get-tuple-element.1679), channel_id=1, replica_groups=mesh['px'=4,'py'=4,'pz'=2] {'px'}, use_global_device_ids=true, to_apply=%region_58.59 | all-reduce | flops 19 | bytes 152 | tf_op jit(solution)/shard_map/psum | solution.py:137
  375.5 3.9 collective-permute-start.24
  381.2 3.7 collective-permute-done.25
  385.0 3.4 collective-permute-start.26
  389.7 6.1 collective-permute-done.27
  403.0 12.6 %all-reduce.12 = (f32[16]{0:T(128)S(1)}, f32[3]{0:T(128)S(1)}, f32[]{:T(128)}) all-reduce(f32[16]{0:T(128)S(1)} %convolution_bitcast_fusion.15, f32[3]{0:T(128)S(1)} %convolution_bitcast_fusion.16, f32[]{:T(128)} %get-tuple-element.1717), channel_id=1, replica_groups=mesh['px'=4,'py'=4,'pz'=2] {'py','pz'}, use_global_device_ids=true, to_apply=%region_64.65 | all-reduce | flops 20 | bytes 160 | tf_op jit(solution)/shard_map/psum | solution.py:138
  415.6 9.0 %all-reduce.20 = (f32[16]{0:T(128)S(1)}, f32[3]{0:T(128)S(1)}, f32[]{:T(128)}) all-reduce(f32[16]{0:T(128)S(1)} %get-tuple-element.1674, f32[3]{0:T(128)S(1)} %get-tuple-element.1675, f32[]{:T(128)} %get-tuple-element.1676), channel_id=1, replica_groups=mesh['px'=4,'py'=4,'pz'=2] {'px'}, use_global_device_ids=true, to_apply=%region_65.66 | all-reduce | flops 20 | bytes 160 | tf_op jit(solution)/shard_map/psum | solution.py:137
  428.6 3.9 collective-permute-start.30
  433.9 4.2 collective-permute-done.31
  438.2 3.5 collective-permute-start.32
  456.3 14.7 %all-reduce.11 = (f32[16]{0:T(128)S(1)}, f32[4]{0:T(128)S(1)}, f32[]{:T(128)}) all-reduce(f32[16]{0:T(128)S(1)} %convolution_bitcast_fusion.13, f32[4]{0:T(128)S(1)} %convolution_bitcast_fusion.14, f32[]{:T(128)} %get-tuple-element.1715), channel_id=1, replica_groups=mesh['px'=4,'py'=4,'pz'=2] {'py','pz'}, use_global_device_ids=true, to_apply=%region_71.72 | all-reduce | flops 21 | bytes 168 | tf_op jit(solution)/shard_map/psum | solution.py:138
  471.0 9.0 %all-reduce.19 = (f32[16]{0:T(128)S(1)}, f32[4]{0:T(128)S(1)}, f32[]{:T(128)}) all-reduce(f32[16]{0:T(128)S(1)} %get-tuple-element.1671, f32[4]{0:T(128)S(1)} %get-tuple-element.1672, f32[]{:T(128)} %get-tuple-element.1673), channel_id=1, replica_groups=mesh['px'=4,'py'=4,'pz'=2] {'px'}, use_global_device_ids=true, to_apply=%region_72.73 | all-reduce | flops 21 | bytes 168 | tf_op jit(solution)/shard_map/psum | solution.py:137
  483.8 3.9 collective-permute-start.36
  509.3 14.2 %all-reduce.10 = (f32[16]{0:T(128)S(1)}, f32[5]{0:T(128)S(1)}, f32[]{:T(128)}) all-reduce(f32[16]{0:T(128)S(1)} %convolution_bitcast_fusion.11, f32[5]{0:T(128)S(1)} %convolution_bitcast_fusion.12, f32[]{:T(128)} %get-tuple-element.1713), channel_id=1, replica_groups=mesh['px'=4,'py'=4,'pz'=2] {'py','pz'}, use_global_device_ids=true, to_apply=%region_78.79 | all-reduce | flops 22 | bytes 176 | tf_op jit(solution)/shard_map/psum | solution.py:138
  523.5 9.0 %all-reduce.18 = (f32[16]{0:T(128)S(1)}, f32[5]{0:T(128)S(1)}, f32[]{:T(128)}) all-reduce(f32[16]{0:T(128)S(1)} %get-tuple-element.1668, f32[5]{0:T(128)S(1)} %get-tuple-element.1669, f32[]{:T(128)} %get-tuple-element.1670), channel_id=1, replica_groups=mesh['px'=4,'py'=4,'pz'=2] {'px'}, use_global_device_ids=true, to_apply=%region_79.80 | all-reduce | flops 22 | bytes 176 | tf_op jit(solution)/shard_map/psum | solution.py:137
  536.5 3.9 collective-permute-start.42
  549.8 5.4 collective-permute-done.45
  564.0 13.6 %all-reduce.9 = (f32[16]{0:T(128)S(1)}, f32[6]{0:T(128)S(1)}, f32[]{:T(128)}) all-reduce(f32[16]{0:T(128)S(1)} %convolution_bitcast_fusion.9, f32[6]{0:T(128)S(1)} %convolution_bitcast_fusion.10, f32[]{:T(128)} %get-tuple-element.1711), channel_id=1, replica_groups=mesh['px'=4,'py'=4,'pz'=2] {'py','pz'}, use_global_device_ids=true, to_apply=%region_85.86 | all-reduce | flops 23 | bytes 184 | tf_op jit(solution)/shard_map/psum | solution.py:138
  577.6 11.3 %all-reduce.17 = (f32[16]{0:T(128)S(1)}, f32[6]{0:T(128)S(1)}, f32[]{:T(128)}) all-reduce(f32[16]{0:T(128)S(1)} %get-tuple-element.1665, f32[6]{0:T(128)S(1)} %get-tuple-element.1666, f32[]{:T(128)} %get-tuple-element.1667), channel_id=1, replica_groups=mesh['px'=4,'py'=4,'pz'=2] {'px'}, use_global_device_ids=true, to_apply=%region_86.87 | all-reduce | flops 23 | bytes 184 | tf_op jit(solution)/shard_map/psum | solution.py:137
  596.4 3.7 collective-permute-done.49
  600.1 3.3 collective-permute-start.50
  618.1 14.2 %all-reduce.8 = (f32[16]{0:T(128)S(1)}, f32[7]{0:T(128)S(1)}, f32[]{:T(128)}) all-reduce(f32[16]{0:T(128)S(1)} %convolution_bitcast_fusion.7, f32[7]{0:T(128)S(1)} %convolution_bitcast_fusion.8, f32[]{:T(128)} %get-tuple-element.1709), channel_id=1, replica_groups=mesh['px'=4,'py'=4,'pz'=2] {'py','pz'}, use_global_device_ids=true, to_apply=%region_92.93 | all-reduce | flops 24 | bytes 192 | tf_op jit(solution)/shard_map/psum | solution.py:138
  632.3 9.5 %all-reduce.16 = (f32[16]{0:T(128)S(1)}, f32[7]{0:T(128)S(1)}, f32[]{:T(128)}) all-reduce(f32[16]{0:T(128)S(1)} %get-tuple-element.1662, f32[7]{0:T(128)S(1)} %get-tuple-element.1663, f32[]{:T(128)} %get-tuple-element.1664), channel_id=1, replica_groups=mesh['px'=4,'py'=4,'pz'=2] {'px'}, use_global_device_ids=true, to_apply=%region_93.94 | all-reduce | flops 24 | bytes 192 | tf_op jit(solution)/shard_map/psum | solution.py:137
  645.9 3.3 collective-permute-start.54
  658.6 5.4 collective-permute-done.57
  672.9 13.6 %all-reduce.7 = (f32[16]{0:T(128)S(1)}, f32[8]{0:T(128)S(1)}, f32[]{:T(128)}) all-reduce(f32[16]{0:T(128)S(1)} %convolution_bitcast_fusion.5, f32[8]{0:T(128)S(1)} %convolution_bitcast_fusion.6, f32[]{:T(128)} %get-tuple-element.1707), channel_id=1, replica_groups=mesh['px'=4,'py'=4,'pz'=2] {'py','pz'}, use_global_device_ids=true, to_apply=%region_99.100 | all-reduce | flops 25 | bytes 200 | tf_op jit(solution)/shard_map/psum | solution.py:138
  686.4 10.9 %all-reduce.15 = (f32[16]{0:T(128)S(1)}, f32[8]{0:T(128)S(1)}, f32[]{:T(128)}) all-reduce(f32[16]{0:T(128)S(1)} %get-tuple-element.1659, f32[8]{0:T(128)S(1)} %get-tuple-element.1660, f32[]{:T(128)} %get-tuple-element.1661), channel_id=1, replica_groups=mesh['px'=4,'py'=4,'pz'=2] {'px'}, use_global_device_ids=true, to_apply=%region_100.101 | all-reduce | flops 25 | bytes 200 | tf_op jit(solution)/shard_map/psum | solution.py:137
  (657 shorter events, 257.5 us)
Async XLA Ops:
  3.0 34.8 %collective-permute-start.6 = (f32[34,1,16,128]{3,0,2,1:T(8,128)S(1)}, f32[34,1,16,128]{3,0,2,1:T(8,128)S(1)}, u32[]{:S(2)}, u32[]{:S(2)}) collective-permute-start(f32[34,1,16,128]{3,0,2,1:T(8,128)S(1)} %get-tuple-element.1735), channel_id=1, source_target_pairs={{0,8},{8,16},{16,24},{1,9},{9,17},{17,25},{2,10},{10,18},{18,26},{... | collective-permute-start | bytes 835592 | tf_op jit(solution)/shard_map/ppermute | solution.py:20
  8.0 29.9 %collective-permute-start.7 = (f32[34,1,16,128]{3,0,2,1:T(8,128)S(1)}, f32[34,1,16,128]{3,0,2,1:T(8,128)S(1)}, u32[]{:S(2)}, u32[]{:S(2)}) collective-permute-start(f32[34,1,16,128]{3,0,2,1:T(8,128)S(1)} %get-tuple-element.1736), channel_id=1, source_target_pairs={{8,0},{16,8},{24,16},{9,1},{17,9},{25,17},{10,2},{18,10},{26,18},{... | collective-permute-start | bytes 835592 | tf_op jit(solution)/shard_map/ppermute | solution.py:21
  9.3 10.0 %collective-permute-start = (f32[1,16,128]{2,1,0:T(8,128)S(1)}, f32[1,16,128]{2,1,0:T(8,128)S(1)}, u32[]{:S(2)}, u32[]{:S(2)}) collective-permute-start(f32[1,16,128]{2,1,0:T(8,128)S(1)} %get-tuple-element.1792), channel_id=1, source_target_pairs={{0,8},{8,16},{16,24},{1,9},{9,17},{17,25},{2,10},{10,18},{18,26},{... | collective-permute-start | bytes 24584 | tf_op jit(solution)/shard_map/ppermute | solution.py:20
  13.9 5.5 collective-permute-start.1
  19.5 12.8 %collective-permute-start.2 = (f32[6,1,128]{2,1,0:T(1,128)S(1)}, f32[6,1,128]{2,1,0:T(1,128)S(1)}, u32[]{:S(2)}, u32[]{:S(2)}) collective-permute-start(f32[6,1,128]{2,1,0:T(1,128)S(1)} %get-tuple-element.1787), channel_id=1, source_target_pairs={{0,2},{2,4},{4,6},{1,3},{3,5},{5,7},{8,10},{10,12},{12,14},{9,11},... | collective-permute-start | bytes 9224 | tf_op jit(solution)/shard_map/ppermute | solution.py:20
  22.9 9.4 %collective-permute-start.3 = (f32[6,1,128]{2,1,0:T(1,128)S(1)}, f32[6,1,128]{2,1,0:T(1,128)S(1)}, u32[]{:S(2)}, u32[]{:S(2)}) collective-permute-start(f32[6,1,128]{2,1,0:T(1,128)S(1)} %get-tuple-element.1788), channel_id=1, source_target_pairs={{2,0},{4,2},{6,4},{3,1},{5,3},{7,5},{10,8},{12,10},{14,12},{11,9},... | collective-permute-start | bytes 9224 | tf_op jit(solution)/shard_map/ppermute | solution.py:21
  32.4 5.3 collective-permute-start.4
  33.7 4.0 collective-permute-start.5
  37.9 8.1 %collective-permute-start.8 = (f32[34,6,1,128]{3,0,2,1:T(8,128)S(1)}, f32[34,6,1,128]{3,0,2,1:T(8,128)S(1)}, u32[]{:S(2)}, u32[]{:S(2)}) collective-permute-start(f32[34,6,1,128]{3,0,2,1:T(8,128)S(1)} %get-tuple-element.1733), channel_id=1, source_target_pairs={{0,2},{2,4},{4,6},{1,3},{3,5},{5,7},{8,10},{10,12},{12,14},{9,11},... | collective-permute-start | bytes 313352 | tf_op jit(solution)/shard_map/ppermute | solution.py:20
  42.5 9.0 %collective-permute-start.9 = (f32[34,6,1,128]{3,0,2,1:T(8,128)S(1)}, f32[34,6,1,128]{3,0,2,1:T(8,128)S(1)}, u32[]{:S(2)}, u32[]{:S(2)}) collective-permute-start(f32[34,6,1,128]{3,0,2,1:T(8,128)S(1)} %get-tuple-element.1734), channel_id=1, source_target_pairs={{2,0},{4,2},{6,4},{3,1},{5,3},{7,5},{10,8},{12,10},{14,12},{11,9},... | collective-permute-start | bytes 313352 | tf_op jit(solution)/shard_map/ppermute | solution.py:21
  58.2 8.5 %collective-permute-start.10 = (f32[34,6,18,1]{0,3,2,1:T(1,128)}, f32[34,6,18,1]{0,3,2,1:T(1,128)}, u32[]{:S(2)}, u32[]{:S(2)}) collective-permute-start(f32[34,6,18,1]{0,3,2,1:T(1,128)} %copy.40), channel_id=1, source_target_pairs={{0,1},{2,3},{4,5},{6,7},{8,9},{10,11},{12,13},{14,15},{16,17},{18,... | collective-permute-start | bytes 44072 | tf_op jit(solution)/shard_map/ppermute | solution.py:20
  63.9 5.9 collective-permute-start.11
  269.2 5.5 collective-permute-start.12
  272.8 5.6 collective-permute-start.13
  278.5 5.5 collective-permute-start.14
  282.7 5.5 collective-permute-start.15
  288.3 3.9 collective-permute-start.16
  323.4 3.9 collective-permute-start.18
  325.9 5.6 collective-permute-start.19
  331.6 5.1 collective-permute-start.20
  334.7 7.4 collective-permute-start.21
  375.5 5.8 collective-permute-start.24
  379.3 5.6 collective-permute-start.25
  385.0 4.7 collective-permute-start.26
  388.4 7.5 collective-permute-start.27
  428.6 5.3 collective-permute-start.30
  432.5 5.6 collective-permute-start.31
  438.2 8.8 %collective-permute-start.32 = (f32[2,6,1,128]{3,2,1,0:T(1,128)S(1)}, f32[2,6,1,128]{3,2,1,0:T(1,128)S(1)}, u32[]{:S(2)}, u32[]{:S(2)}) collective-permute-start(f32[2,6,1,128]{3,2,1,0:T(1,128)S(1)} %get-tuple-element.1761), channel_id=1, source_target_pairs={{0,2},{2,4},{4,6},{1,3},{3,5},{5,7},{8,10},{10,12},{12,14},{9,11},... | collective-permute-start | bytes 18440 | tf_op jit(solution)/shard_map/ppermute | solution.py:20
  441.7 7.4 collective-permute-start.33
  483.8 6.7 collective-permute-start.36
  487.7 5.6 collective-permute-start.37
  493.3 6.4 collective-permute-start.38
  494.8 7.4 collective-permute-start.39
  536.5 9.1 %collective-permute-start.42 = (f32[2,1,16,128]{3,2,1,0:T(8,128)S(1)}, f32[2,1,16,128]{3,2,1,0:T(8,128)S(1)}, u32[]{:S(2)}, u32[]{:S(2)}) collective-permute-start(f32[2,1,16,128]{3,2,1,0:T(8,128)S(1)} %get-tuple-element.1775), channel_id=1, source_target_pairs={{0,8},{8,16},{16,24},{1,9},{9,17},{17,25},{2,10},{10,18},{18,26},{... | collective-permute-start | bytes 49160 | tf_op jit(solution)/shard_map/ppermute | solution.py:20
  540.3 5.6 collective-permute-start.43
  546.0 3.8 collective-permute-start.44
  547.8 7.4 collective-permute-start.45
  555.3 6.3 collective-permute-start.46
  556.6 5.0 collective-permute-start.47
  594.5 5.6 collective-permute-start.49
  600.1 8.3 %collective-permute-start.50 = (f32[2,6,1,128]{3,2,1,0:T(1,128)S(1)}, f32[2,6,1,128]{3,2,1,0:T(1,128)S(1)}, u32[]{:S(2)}, u32[]{:S(2)}) collective-permute-start(f32[2,6,1,128]{3,2,1,0:T(1,128)S(1)} %get-tuple-element.1755), channel_id=1, source_target_pairs={{0,2},{2,4},{4,6},{1,3},{3,5},{5,7},{8,10},{10,12},{12,14},{9,11},... | collective-permute-start | bytes 18440 | tf_op jit(solution)/shard_map/ppermute | solution.py:20
  603.4 7.5 collective-permute-start.51
  645.9 8.2 %collective-permute-start.54 = (f32[2,1,16,128]{3,2,1,0:T(8,128)S(1)}, f32[2,1,16,128]{3,2,1,0:T(8,128)S(1)}, u32[]{:S(2)}, u32[]{:S(2)}) collective-permute-start(f32[2,1,16,128]{3,2,1,0:T(8,128)S(1)} %get-tuple-element.1771), channel_id=1, source_target_pairs={{0,8},{8,16},{16,24},{1,9},{9,17},{17,25},{2,10},{10,18},{18,26},{... | collective-permute-start | bytes 49160 | tf_op jit(solution)/shard_map/ppermute | solution.py:20
  649.2 5.6 collective-permute-start.55
  654.8 3.8 collective-permute-start.56
  656.7 7.4 collective-permute-start.57
  664.2 6.3 collective-permute-start.58
  665.5 5.0 collective-permute-start.59
  (46 other events, 1985.6 us)
